TPU v7x, 128 devices: a whole 4x4x4 slice. The times are simulated.
128 devices in a mesh: rep: 1, dp: 128 (over x, y, z, core).
Axes of the slice: x: 4, y: 4, z: 4, core: 2. Of those that a mesh axis runs over, the one named last changes fastest.
Arguments:
- a: bfloat16 [128, 2, 4096, 1280], P(('rep', 'dp'))
- g: bfloat16 [128, 2, 4096, 3584], P(('rep', 'dp'))
Outputs:
- output: bfloat16 [2, 1280, 3584], P('rep')
All inputs are finite; a program needn't handle non-finite values.
Results may differ from a plain program's by a relative error of at most 0.012.
Values are sent between devices in bfloat16 or wider.
A program may use at most 1.5 GiB of HBM per device.

v0:
```python
import jax
import jax.numpy as jnp


def solution(mesh):
    groups = mesh.shape["rep"]

    def step(a, g):
        a, g = (t.reshape(groups, -1, *t.shape[1:]) for t in (a, g))
        sums = jnp.einsum("rsntd,rsntf->rndf", a, g, preferred_element_type=jnp.float32)
        return sums.astype(jnp.bfloat16).reshape(-1, *sums.shape[2:])

    return step
```

profile of v0, /device:TPU:1, one launch (start us, length us, event | category | flops | bytes accessed | tf_op | source)
XLA Modules:
  0.0 293.1 jit_solution(12748756789662866115)
XLA Ops:
  0.0 86.4 %fusion = f32[2,1280,3584]{2,1,0:T(8,128)} fusion(bf16[1,2,4096,3584]{3,2,1,0:T(8,128)(2,1)} %param.1, bf16[1,2,4096,1280]{3,2,1,0:T(8,128)(2,1)} %param), kind=kOutput, calls=%fused_computation | convolution fusion | flops 75161927680 | bytes 116391936 | tf_op jit(solution)/rsntd,rsntf->rndf/dot_general | solution.py:10
  86.4 206.7 %all-reduce.2 = bf16[2,1280,3584]{2,1,0:T(8,128)(2,1)} all-reduce(f32[2,1280,3584]{2,1,0:T(8,128)} %fusion), channel_id=1, replica_groups=mesh['axis_0'=128] {'axis_0'}, use_global_device_ids=true, to_apply=%add.clone | all-reduce | flops 9175040 | bytes 55050240 | tf_op jit(solution)/rsntd,rsntf->rndf/dot_general | solution.py:10
where the time goes:
time: 294 us; the launch traced here: 293 us
  blocking collectives  207 us (70%)
  matrix products  86.4 us (29%)
    dot_general x1, blocking collectives, step(): jnp.einsum('rsntd,rsntf->rndf', a, g, preferred_element_type=jnp.float32)  207 us
    dot_general x1, matrix products, step(): jnp.einsum('rsntd,rsntf->rndf', a, g, preferred_element_type=jnp.float32)  86.4 us

commit v1 on v0

v1 whole, which is shorter than its diff:
```python
import jax
import jax.numpy as jnp
from jax import lax
from jax.experimental import pallas as pl
from jax.experimental.pallas import tpu as pltpu
from jax.sharding import PartitionSpec as P

N, D, F, K = 2, 1280, 3584, 4096
NB = 512
NC = F // NB
CH = N * NC
H = D // 2
RB = H // 4
CB = NB // 4
HB = RB // 2
HC = NB // 2

F32, BF16 = jnp.float32, jnp.bfloat16

OFF = {2: 2, 3: 5, 4: 7, 5: 9, 6: 11, 7: 13, 8: 15, 9: 17, 10: 20, 11: 22}
LAST = CH + (OFF[11] + 1) // 2 + 1


def kernel(a_ref, g_ref, out, av, gv, fs, fb, d2d, ra1, ra2, rb1, rb2, rc,
           sem_a, sem_g, s_d, r_d, s_x, r_d2, ss, rs, free):
    me = lax.axis_index("dp")
    core = me % 2
    partner = me + 1 - 2 * core
    mine = pl.multiple_of(core * H, H)
    theirs = pl.multiple_of((1 - core) * H, H)

    def axis(k):
        stride = 32 - 33 * k + 9 * k * k
        return (me // stride) % 4, stride

    def dev(k, d):
        c, stride = axis(k)
        return me + ((c + d + 4) % 4 - c) * stride

    def rdma(src, dst, s, r, to):
        return pltpu.make_async_remote_copy(
            src_ref=src, dst_ref=dst, send_sem=s, recv_sem=r,
            device_id={"dp": to}, device_id_type=pl.DeviceIdType.MESH)

    def acopy(n):
        return pltpu.make_async_copy(a_ref.at[0, n], av.at[n], sem_a.at[n])

    def gcopy(t):
        n, c = t // NC, t % NC
        cols = pl.ds(pl.multiple_of(c * NB, NB), NB)
        return pltpu.make_async_copy(g_ref.at[0, n, :, cols], gv.at[t % 2], sem_g.at[t % 2])

    acopy(0).start()
    gcopy(0).start()
    acopy(1).start()

    barrier = pltpu.get_barrier_semaphore()
    pl.semaphore_signal(barrier, inc=1, device_id={"dp": partner}, device_id_type=pl.DeviceIdType.MESH)
    for k in range(3):
        for d in (1, -1):
            pl.semaphore_signal(barrier, inc=1, device_id={"dp": dev(k, d)},
                                device_id_type=pl.DeviceIdType.MESH)
    pl.semaphore_wait(barrier, 7)

    acopy(0).wait()

    def dot(n, t, rows):
        return lax.dot_general(av[n, :, pl.ds(rows, H)], gv[t % 2], (((0,), (0,)), ((), ())),
                               preferred_element_type=F32)

    class Chunk:
        def __init__(self, t):
            self.t = t
            self.n, c = t // NC, t % NC
            self.col = pl.multiple_of(c * NB, NB)
            self.r = t % 3
            self.s3, self.s6 = t % 3, t % 6

        def ax(self, i):
            return (self.r + i) % 3

        def pos(self, i, d):
            return (axis(self.ax(i))[0] + d + 4) % 4

        def dev(self, i, d):
            return dev(self.ax(i), d)

        def block(self, d, half=None):
            rows = pl.ds(pl.multiple_of(mine + self.pos(0, d) * RB, RB), RB)
            if half is None:
                return out.at[self.n, rows, pl.ds(self.col, NB)]
            return out.at[self.n, rows, pl.ds(pl.multiple_of(self.col + half * HC, HC), HC)]

        def rel(self, d):
            return pl.ds(pl.multiple_of(self.pos(0, d) * RB, RB), RB)

        def sub(self, d, half=None):
            r0 = mine + self.pos(0, 0) * RB
            cols = pl.ds(pl.multiple_of(self.col + self.pos(1, d) * CB, CB), CB)
            if half is None:
                return out.at[self.n, pl.ds(pl.multiple_of(r0, RB), RB), cols]
            return out.at[self.n, pl.ds(pl.multiple_of(r0 + half * HB, HB), HB), cols]

        def relc(self, d):
            return pl.ds(pl.multiple_of(self.pos(1, d) * CB, CB), CB)

        def copies(self, st):
            s3, s6 = self.s3, self.s6
            if st == 1:
                i, p = 0, ((self.block(2, 0), ra1.at[s3, 0]), (self.block(2, 1), ra1.at[s3, 1]))
            elif st == 2:
                i, p = 0, ((self.block(1), ra2.at[s3, 0]), (self.block(-1), ra2.at[s3, 1]))
            elif st == 3:
                i, p = 1, ((self.sub(2, 0), rb1.at[s3, 0]), (self.sub(2, 1), rb1.at[s3, 1]))
            elif st == 4:
                i, p = 1, ((self.sub(1), rb2.at[s3, 0]), (self.sub(-1), rb2.at[s3, 1]))
            elif st == 5:
                i, p = 2, ((self.sub(0), rc.at[s6, 0]), (self.sub(0), rc.at[s6, 1]))
            elif st == 6:
                up, lo = pl.ds(0, HB), pl.ds(HB, HB)
                i, p = 2, ((rc.at[s6, 0, up], rc.at[s6, 2, up]), (rc.at[s6, 1, lo], rc.at[s6, 2, lo]))
            elif st == 7:
                i, p = 1, ((self.sub(0), self.sub(0)), (self.sub(0), self.sub(0)))
            elif st == 8:
                i, p = 1, ((self.sub(-1, 0), self.sub(-1, 0)), (self.sub(1, 1), self.sub(1, 1)))
            elif st == 9:
                i, p = 0, ((self.block(0), self.block(0)), (self.block(0), self.block(0)))
            elif st == 10:
                i, p = 0, ((self.block(-1, 0), self.block(-1, 0)), (self.block(1, 1), self.block(1, 1)))
            return [rdma(src, dst, ss.at[st - 1, j, s6], rs.at[st - 1, j, s6], self.dev(i, d))
                    for j, (d, (src, dst)) in enumerate(zip((1, -1), p))]

        def send(self, st):
            for c in self.copies(st):
                c.start()

        def wait(self, st):
            for c in self.copies(st):
                c.wait_send()
            for c in self.copies(st):
                c.wait_recv()

        def send_theirs(self):
            src = out.at[self.n, pl.ds(theirs, H), pl.ds(self.col, NB)]
            return rdma(src, d2d.at[self.t % 5], s_d.at[self.t % 5], r_d.at[self.t % 5], partner)

        def send_mine(self):
            src = out.at[self.n, pl.ds(mine, H), pl.ds(self.col, NB)]
            return rdma(src, src, s_x.at[self.t], r_d2.at[self.t], partner)

        def give(self, i):
            for j, d in enumerate((1, -1)):
                pl.semaphore_signal(free.at[i, j, self.s6], inc=1, device_id={"dp": self.dev(i, d)},
                                    device_id_type=pl.DeviceIdType.MESH)

        def take(self, i):
            for j in range(2):
                pl.semaphore_wait(free.at[i, j, self.s6], 1)

        def chip(self, d):
            rows = self.rel(d)
            return fs[self.s3, rows, :] + d2d[self.t % 5, rows, :].astype(F32)

        def stage(self, st):
            self.wait(st - 1)
            s3, s6 = self.s3, self.s6
            if st == 2:
                v = self.chip(1)
                self.block(1, 0)[...] = (v[:, :HC] + ra1[s3, 0].astype(F32)).astype(BF16)
                self.block(1, 1)[...] = v[:, HC:].astype(BF16)
                v = self.chip(-1)
                self.block(-1, 0)[...] = v[:, :HC].astype(BF16)
                self.block(-1, 1)[...] = (v[:, HC:] + ra1[s3, 1].astype(F32)).astype(BF16)
            elif st == 3:
                fb[s3] = self.chip(0) + ra2[s3, 0].astype(F32) + ra2[s3, 1].astype(F32)
                self.sub(2)[...] = fb[s3, :, self.relc(2)].astype(BF16)
            elif st == 4:
                v = fb[s3, :, self.relc(1)]
                self.sub(1, 0)[...] = (v[:HB] + rb1[s3, 0].astype(F32)).astype(BF16)
                self.sub(1, 1)[...] = v[HB:].astype(BF16)
                v = fb[s3, :, self.relc(-1)]
                self.sub(-1, 0)[...] = v[:HB].astype(BF16)
                self.sub(-1, 1)[...] = (v[HB:] + rb1[s3, 1].astype(F32)).astype(BF16)
            elif st == 5:
                v = fb[s3, :, self.relc(0)]
                self.sub(0)[...] = (v + rb2[s3, 0].astype(F32) + rb2[s3, 1].astype(F32)).astype(BF16)
            elif st == 7:
                even = self.sub(0)[...].astype(F32) + rc[s6, 2].astype(F32)
                odd = rc[s6, 0].astype(F32) + rc[s6, 1].astype(F32)
                self.sub(0)[...] = (even + odd).astype(BF16)
            if st == 3:
                self.give(0)
            elif st == 5:
                self.give(1)
            elif st == 7:
                self.take(1)
            elif st == 9:
                self.take(0)
            if st <= 10:
                self.send(st)
            else:
                pl.semaphore_wait(free.at[2, 0, s6], 1)
                self.send_mine().start()

    def slot(t, half):
        for st in range(11, 1, -1):
            off = OFF[st]
            if half == 1 and off % 2 == 0:
                u = t - off // 2
            elif half == 0 and off % 2 == 1:
                u = t - (1 + off) // 2
            else:
                continue

            @pl.when(jnp.logical_and(u >= 0, u < CH))
            def _():
                Chunk(u).stage(st)

    def body(t, _):
        c = Chunk(t)

        @pl.when(t < CH)
        def _():
            @pl.when(t + 1 < CH)
            def _():
                gcopy(t + 1).start()
            gcopy(t).wait()

            @pl.when(t == NC)
            def _():
                acopy(1).wait()

            out[c.n, pl.ds(theirs, H), pl.ds(c.col, NB)] = dot(c.n, t, theirs).astype(BF16)
            c.send_theirs().start()

        slot(t, 0)

        @pl.when(t < CH)
        def _():
            fs[c.s3] = dot(c.n, t, mine)
            w = c.send_theirs()
            w.wait_send()
            pl.semaphore_signal(free.at[2, 0, c.s6], inc=1, device_id={"dp": partner},
                                device_id_type=pl.DeviceIdType.MESH)
            w.wait_recv()
            c.block(2)[...] = c.chip(2).astype(BF16)
            c.send(1)

        slot(t, 1)
        return 0

    lax.fori_loop(0, LAST, body, 0)

    def drain(t, _):
        c = Chunk(t).send_mine()
        c.wait_send()
        c.wait_recv()
        return 0

    lax.fori_loop(0, CH, drain, 0)


def local(a, g):
    dma = pltpu.SemaphoreType.DMA
    return pl.pallas_call(
        kernel,
        out_shape=pltpu.VMEM((N, D, F), BF16),
        in_specs=[pl.BlockSpec(memory_space=pl.ANY)] * 2,
        out_specs=pl.BlockSpec(memory_space=pltpu.VMEM),
        scratch_shapes=[
            pltpu.VMEM((N, K, D), BF16),
            pltpu.VMEM((2, K, NB), BF16),
            pltpu.VMEM((3, H, NB), F32),
            pltpu.VMEM((3, RB, NB), F32),
            pltpu.VMEM((5, H, NB), BF16),
            pltpu.VMEM((3, 2, RB, HC), BF16),
            pltpu.VMEM((3, 2, RB, NB), BF16),
            pltpu.VMEM((3, 2, HB, CB), BF16),
            pltpu.VMEM((3, 2, RB, CB), BF16),
            pltpu.VMEM((6, 3, RB, CB), BF16),
            dma((2,)), dma((2,)), dma((5,)), dma((5,)), dma((CH,)), dma((CH,)),
            dma((10, 2, 6)), dma((10, 2, 6)), pltpu.SemaphoreType.REGULAR((3, 2, 6)),
        ],
        compiler_params=pltpu.CompilerParams(
            collective_id=0, has_side_effects=True, vmem_limit_bytes=46 * 2**20),
        name="wgrad_sum",
    )(a, g)


def solution(mesh):
    spec = P(("rep", "dp"))
    return jax.shard_map(local, mesh=mesh, in_specs=(spec, spec), out_specs=P("rep"), check_vma=False)
```

time: 294 us -> 168 us (0.57)
  blocking collectives: 207 us -> 0 us
  Pallas kernels: 0 us -> 161 us
  matrix products: 86.4 us -> 0 us
  local copies, waits for them, and re-layouts: 0 us -> 6.68 us
    dot_general x1 -> x0, blocking collectives: 207 us -> none  [step(): jnp.einsum('rsntd,rsntf->rndf', a, g, preferred_element_type=jnp.float32)]
    pallas_call x0 -> x1, Pallas kernels: none -> 161 us  [local(): pl.pallas_call(kernel, out_shape=pltpu.VMEM((N, D, F), BF16), in_specs=[p...]
    dot_general x1 -> x0, matrix products: 86.4 us -> none  [step(): jnp.einsum('rsntd,rsntf->rndf', a, g, preferred_element_type=jnp.float32)]
    unnamed x0 -> x1, local copies, waits for them, and re-layouts: none -> 6.68 us
where the time goes in v1:
time: 168 us
  Pallas kernels  161 us (96%)
  local copies, waits for them, and re-layouts  6.68 us (4%)
    pallas_call x1, Pallas kernels, local(): pl.pallas_call(kernel, out_shape=pltpu.VMEM((N, D, F), BF16), in_specs=[p...  161 us
    unnamed x1, local copies, waits for them, and re-layouts  6.68 us

profile of v1, /device:TPU:1, one launch (start us, length us, event | category | flops | bytes accessed | tf_op | source)
XLA Modules:
  0.0 167.7 jit_solution(11022152406955030055)
XLA Ops:
  0.0 161.0 %wgrad_sum.1 = bf16[2,1280,3584]{2,1,0:T(8,128)(2,1)S(1)} custom-call(bf16[1,2,4096,1280]{3,2,1,0:T(8,128)(2,1)} %a_ref.1, bf16[1,2,4096,3584]{3,2,1,0:T(8,128)(2,1)} %g_ref.1), custom_call_target="tpu_custom_call" | custom-call | tf_op jit(solution)/shard_map/wgrad_sum/pallas_call | solution.py:265
  161.0 6.7 %copy.4 = bf16[2,1280,3584]{2,1,0:T(8,128)(2,1)} copy(bf16[2,1280,3584]{2,1,0:T(8,128)(2,1)S(1)} %wgrad_sum.1) | data formatting | bytes 36700160

commit v2 on v1

v2 whole, which is shorter than its diff:
```python
import jax
import jax.numpy as jnp
from jax import lax
from jax.experimental import pallas as pl
from jax.experimental.pallas import tpu as pltpu
from jax.sharding import PartitionSpec as P

N, D, F, K = 2, 1280, 3584, 4096
NB = 512
NC = F // NB
CH = N * NC
H = D // 2
RB = H // 4
CB = NB // 4
FC = NB // 4
PEERS = (1, 2, -1)

F32, BF16 = jnp.float32, jnp.bfloat16

OFF = {2: 2, 3: 5, 4: 7, 5: 9, 6: 11, 7: 14, 8: 16}
LAST = CH + (OFF[8] + 1) // 2 + 1


def kernel(a_ref, g_ref, out, av, gv, fs, fb, d2d, ra1, ra2, rb, rc,
           sem_a, sem_g, s_d, r_d, s_x, r_d2, ss, rs, free):
    me = lax.axis_index("dp")
    core = me % 2
    partner = me + 1 - 2 * core
    mine = pl.multiple_of(core * H, H)
    theirs = pl.multiple_of((1 - core) * H, H)

    place, device = [], []
    for stride in (32, 8, 2):
        c = (me // stride) % 4
        place.append({d: (c + d + 4) % 4 for d in (-1, 0, 1, 2)})
        device.append({d: me + (place[-1][d] - c) * stride for d in PEERS})

    def pick(k, of, d):
        return jnp.where(k == 0, of[0][d], jnp.where(k == 1, of[1][d], of[2][d]))

    def rdma(src, dst, s, r, to):
        return pltpu.make_async_remote_copy(
            src_ref=src, dst_ref=dst, send_sem=s, recv_sem=r,
            device_id={"dp": to}, device_id_type=pl.DeviceIdType.MESH)

    def acopy(n, rows):
        cols = pl.ds(rows, H)
        return pltpu.make_async_copy(a_ref.at[0, n, :, cols], av.at[n, :, cols], sem_a.at[n, (0 if rows is theirs else 1)])

    def split(t):
        n = jnp.where(t >= NC, 1, 0)
        return n, t - n * NC

    def gcopy(t):
        n, c = split(t)
        cols = pl.ds(pl.multiple_of(c * NB, NB), NB)
        b = lax.rem(t, 2)
        return pltpu.make_async_copy(g_ref.at[0, n, :, cols], gv.at[b], sem_g.at[b])

    gcopy(0).start()
    acopy(0, theirs).start()
    acopy(0, mine).start()

    barrier = pltpu.get_barrier_semaphore()
    pl.semaphore_signal(barrier, inc=1, device_id={"dp": partner}, device_id_type=pl.DeviceIdType.MESH)
    for k in range(3):
        for d in PEERS:
            pl.semaphore_signal(barrier, inc=1, device_id={"dp": device[k][d]},
                                device_id_type=pl.DeviceIdType.MESH)
    pl.semaphore_wait(barrier, 10)

    def dot(n, t, rows):
        return lax.dot_general(av[n, :, pl.ds(rows, H)], gv[lax.rem(t, 2)], (((0,), (0,)), ((), ())),
                               preferred_element_type=F32)

    class Chunk:
        def __init__(self, t, s6):
            self.t = t
            self.n, c = split(t)
            self.col = pl.multiple_of(c * NB, NB)
            self.s6 = s6
            self.s3 = jnp.where(s6 >= 3, s6 - 3, s6)

        def ax(self, i):
            k = self.s3 + core + i
            return jnp.where(k >= 3, k - 3, k)

        def pos(self, i, d):
            return pick(self.ax(i), place, d)

        def dev(self, i, d):
            return pick(self.ax(i), device, d)

        def block(self, d, lo=0, n=NB):
            rows = pl.ds(pl.multiple_of(mine + self.pos(0, d) * RB, RB), RB)
            return out.at[self.n, rows, pl.ds(pl.multiple_of(self.col + lo, CB), n)]

        def rel(self, d):
            return pl.ds(pl.multiple_of(self.pos(0, d) * RB, RB), RB)

        def sub(self, d):
            rows = pl.ds(pl.multiple_of(mine + self.pos(0, 0) * RB, RB), RB)
            return out.at[self.n, rows, pl.ds(pl.multiple_of(self.col + self.pos(1, d) * CB, CB), CB)]

        def relc(self, d):
            return pl.ds(pl.multiple_of(self.pos(1, d) * CB, CB), CB)

        def copies(self, st):
            s3, s6 = self.s3, self.s6
            lo, hi = pl.ds(0, FC), pl.ds(FC, NB - FC)
            if st == 1:
                i, p = 0, ((1, self.block(2, 0, FC), ra1.at[s3, :, lo]),
                           (-1, self.block(2, FC, NB - FC), ra1.at[s3, :, hi]))
            elif st == 2:
                i, p = 0, ((1, self.block(1), ra2.at[s3, 0]), (-1, self.block(-1), ra2.at[s3, 1]))
            elif st == 3:
                i, p = 1, [(d, self.sub(d), rb.at[s3, j]) for j, d in enumerate(PEERS)]
            elif st == 4:
                i, p = 2, [(d, self.sub(0), rc.at[s6, j]) for j, d in enumerate(PEERS)]
            elif st == 5:
                i, p = 1, [(d, self.sub(0), self.sub(0)) for d in PEERS]
            elif st == 6:
                i, p = 0, [(d, self.block(0), self.block(0)) for d in (1, -1)]
            elif st == 7:
                fwd, bwd = self.block(-1, 0, FC), self.block(1, FC, NB - FC)
                i, p = 0, ((1, fwd, fwd), (-1, bwd, bwd))
            return [rdma(src, dst, ss.at[st - 1, j, s6], rs.at[st - 1, j, s6], self.dev(i, d))
                    for j, (d, src, dst) in enumerate(p)]

        def send(self, st):
            for c in self.copies(st):
                c.start()

        def wait(self, st):
            copies = self.copies(st)
            for c in copies:
                c.wait_send()
            for c in copies:
                c.wait_recv()

        def send_theirs(self):
            src = out.at[self.n, pl.ds(theirs, H), pl.ds(self.col, NB)]
            return rdma(src, d2d.at[self.s6], s_d.at[self.s6], r_d.at[self.s6], partner)

        def send_mine(self):
            src = out.at[self.n, pl.ds(mine, H), pl.ds(self.col, NB)]
            return rdma(src, src, s_x.at[self.t], r_d2.at[self.t], partner)

        def give(self, i, peers):
            for j, d in enumerate(peers):
                pl.semaphore_signal(free.at[i, j, self.s6], inc=1, device_id={"dp": self.dev(i, d)},
                                    device_id_type=pl.DeviceIdType.MESH)

        def take(self, i, n):
            for j in range(n):
                pl.semaphore_wait(free.at[i, j, self.s6], 1)

        def chip(self, d):
            rows = self.rel(d)
            return fs[self.s3, rows, :] + d2d[self.s6, rows, :].astype(F32)

        def stage(self, st):
            self.wait(st - 1)
            s3, s6 = self.s3, self.s6
            if st == 2:
                v = self.chip(1)
                self.block(1, 0, FC)[...] = (v[:, :FC] + ra1[s3, :, :FC].astype(F32)).astype(BF16)
                self.block(1, FC, NB - FC)[...] = v[:, FC:].astype(BF16)
                v = self.chip(-1)
                self.block(-1, 0, FC)[...] = v[:, :FC].astype(BF16)
                self.block(-1, FC, NB - FC)[...] = (v[:, FC:] + ra1[s3, :, FC:].astype(F32)).astype(BF16)
            elif st == 3:
                fb[s3] = self.chip(0) + ra2[s3, 0].astype(F32) + ra2[s3, 1].astype(F32)
                for d in PEERS:
                    self.sub(d)[...] = fb[s3, :, self.relc(d)].astype(BF16)
                self.give(0, (1, -1))
            elif st == 4:
                v = fb[s3, :, self.relc(0)]
                for j in range(3):
                    v = v + rb[s3, j].astype(F32)
                self.sub(0)[...] = v.astype(BF16)
                self.give(1, PEERS)
            elif st == 5:
                even = self.sub(0)[...].astype(F32) + rc[s6, 1].astype(F32)
                odd = rc[s6, 0].astype(F32) + rc[s6, 2].astype(F32)
                self.sub(0)[...] = (even + odd).astype(BF16)
                self.take(1, 3)
            elif st == 6:
                self.take(0, 2)
            if st <= 7:
                self.send(st)
            else:
                pl.semaphore_wait(free.at[2, 0, s6], 1)
                self.send_mine().start()

    def slot(t, t6, half):
        for st in range(8, 1, -1):
            off = OFF[st]
            if half == 1 and off % 2 == 0:
                back = off // 2
            elif half == 0 and off % 2 == 1:
                back = (1 + off) // 2
            else:
                continue
            u, u6 = t - back, t6 - back % 6

            @pl.when(jnp.logical_and(u >= 0, u < CH))
            def _():
                Chunk(u, jnp.where(u6 < 0, u6 + 6, u6)).stage(st)

    def body(t, t6):
        c = Chunk(t, t6)

        @pl.when(t < CH)
        def _():
            @pl.when(t + 1 < CH)
            def _():
                gcopy(t + 1).start()
            gcopy(t).wait()

            @pl.when(c.col == 0)
            def _():
                acopy(c.n, theirs).wait()

            out[c.n, pl.ds(theirs, H), pl.ds(c.col, NB)] = dot(c.n, t, theirs).astype(BF16)
            c.send_theirs().start()

        slot(t, t6, 0)

        @pl.when(t < CH)
        def _():
            @pl.when(c.col == 0)
            def _():
                acopy(c.n, mine).wait()

            @pl.when(t == 1)
            def _():
                acopy(1, theirs).start()
                acopy(1, mine).start()

            fs[c.s3] = dot(c.n, t, mine)
            w = c.send_theirs()
            w.wait_send()
            pl.semaphore_signal(free.at[2, 0, c.s6], inc=1, device_id={"dp": partner},
                                device_id_type=pl.DeviceIdType.MESH)
            w.wait_recv()
            c.block(2)[...] = c.chip(2).astype(BF16)
            c.send(1)

        slot(t, t6, 1)
        return jnp.where(t6 == 5, 0, t6 + 1)

    lax.fori_loop(0, LAST, body, 0)

    def drain(t, _):
        c = Chunk(t, 0).send_mine()
        c.wait_send()
        c.wait_recv()
        return 0

    lax.fori_loop(0, CH, drain, 0)


def local(a, g):
    dma = pltpu.SemaphoreType.DMA
    return pl.pallas_call(
        kernel,
        out_shape=pltpu.VMEM((N, D, F), BF16),
        in_specs=[pl.BlockSpec(memory_space=pl.ANY)] * 2,
        out_specs=pl.BlockSpec(memory_space=pltpu.VMEM),
        scratch_shapes=[
            pltpu.VMEM((N, K, D), BF16),
            pltpu.VMEM((2, K, NB), BF16),
            pltpu.VMEM((3, H, NB), F32),
            pltpu.VMEM((3, RB, NB), F32),
            pltpu.VMEM((6, H, NB), BF16),
            pltpu.VMEM((3, RB, NB), BF16),
            pltpu.VMEM((3, 2, RB, NB), BF16),
            pltpu.VMEM((3, 3, RB, CB), BF16),
            pltpu.VMEM((6, 3, RB, CB), BF16),
            dma((2, 2)), dma((2,)), dma((6,)), dma((6,)), dma((CH,)), dma((CH,)),
            dma((7, 3, 6)), dma((7, 3, 6)), pltpu.SemaphoreType.REGULAR((3, 3, 6)),
        ],
        compiler_params=pltpu.CompilerParams(
            collective_id=0, has_side_effects=True, vmem_limit_bytes=46 * 2**20),
        name="wgrad_sum",
    )(a, g)


def solution(mesh):
    spec = P(("rep", "dp"))
    return jax.shard_map(local, mesh=mesh, in_specs=(spec, spec), out_specs=P("rep"), check_vma=False)
```

time: 168 us -> 152 us (0.905)
  Pallas kernels: 161 us -> 145 us
    pallas_call x1, Pallas kernels: 161 us -> 145 us  [local(): pl.pallas_call(kernel, out_shape=pltpu.VMEM((N, D, F), BF16), in_specs=[p...]
where the time goes in v2:
time: 152 us
  Pallas kernels  145 us (95%)
  local copies, waits for them, and re-layouts  6.68 us (4%)
    pallas_call x1, Pallas kernels, local(): pl.pallas_call(kernel, out_shape=pltpu.VMEM((N, D, F), BF16), in_specs=[p...  145 us
    unnamed x1, local copies, waits for them, and re-layouts  6.68 us

profile of v2, /device:TPU:1, one launch (start us, length us, event | category | flops | bytes accessed | tf_op | source)
XLA Modules:
  0.0 151.8 jit_solution(5359051010213301458)
XLA Ops:
  0.0 145.1 %wgrad_sum.1 = bf16[2,1280,3584]{2,1,0:T(8,128)(2,1)S(1)} custom-call(bf16[1,2,4096,1280]{3,2,1,0:T(8,128)(2,1)} %a_ref.1, bf16[1,2,4096,3584]{3,2,1,0:T(8,128)(2,1)} %g_ref.1), custom_call_target="tpu_custom_call" | custom-call | tf_op jit(solution)/shard_map/wgrad_sum/pallas_call | solution.py:266
  145.1 6.7 %copy.4 = bf16[2,1280,3584]{2,1,0:T(8,128)(2,1)} copy(bf16[2,1280,3584]{2,1,0:T(8,128)(2,1)S(1)} %wgrad_sum.1) | data formatting | bytes 36700160

commit v3 on v2

--- a/solution.py
+++ b/solution.py
@@ -14,10 +14,11 @@
 CB = NB // 4
 FC = NB // 4
 PEERS = (1, 2, -1)
+STRIP = 32
 
 F32, BF16 = jnp.float32, jnp.bfloat16
 
-OFF = {2: 2, 3: 5, 4: 7, 5: 9, 6: 11, 7: 14, 8: 16}
+OFF = {2: 2, 3: 5, 4: 7, 5: 9, 6: 11, 7: 13, 8: 15}
 LAST = CH + (OFF[8] + 1) // 2 + 1
 
 
@@ -72,6 +73,14 @@
     def dot(n, t, rows):
         return lax.dot_general(av[n, :, pl.ds(rows, H)], gv[lax.rem(t, 2)], (((0,), (0,)), ((), ())),
                                preferred_element_type=F32)
+
+    def total(dst, *terms):
+        for r in range(0, dst.shape[0], STRIP):
+            rows = pl.ds(r, STRIP)
+            v = terms[0][rows, :].astype(F32)
+            for term in terms[1:]:
+                v = v + term[rows, :].astype(F32)
+            dst[rows, :] = v.astype(dst.dtype)
 
     class Chunk:
         def __init__(self, t, s6):
@@ -155,30 +164,26 @@
             for j in range(n):
                 pl.semaphore_wait(free.at[i, j, self.s6], 1)
 
-        def chip(self, d):
-            rows = self.rel(d)
-            return fs[self.s3, rows, :] + d2d[self.s6, rows, :].astype(F32)
+        def chip(self, d, lo=0, n=NB):
+            rows, cols = self.rel(d), pl.ds(lo, n)
+            return fs.at[self.s3, rows, cols], d2d.at[self.s6, rows, cols]
 
         def stage(self, st):
             self.wait(st - 1)
             s3, s6 = self.s3, self.s6
+            rest = NB - FC
             if st == 2:
-                v = self.chip(1)
-                self.block(1, 0, FC)[...] = (v[:, :FC] + ra1[s3, :, :FC].astype(F32)).astype(BF16)
-                self.block(1, FC, NB - FC)[...] = v[:, FC:].astype(BF16)
-                v = self.chip(-1)
-                self.block(-1, 0, FC)[...] = v[:, :FC].astype(BF16)
-                self.block(-1, FC, NB - FC)[...] = (v[:, FC:] + ra1[s3, :, FC:].astype(F32)).astype(BF16)
+                total(self.block(1, 0, FC), *self.chip(1, 0, FC), ra1.at[s3, :, pl.ds(0, FC)])
+                total(self.block(1, FC, rest), *self.chip(1, FC, rest))
+                total(self.block(-1, 0, FC), *self.chip(-1, 0, FC))
+                total(self.block(-1, FC, rest), *self.chip(-1, FC, rest), ra1.at[s3, :, pl.ds(FC, rest)])
             elif st == 3:
-                fb[s3] = self.chip(0) + ra2[s3, 0].astype(F32) + ra2[s3, 1].astype(F32)
+                total(fb.at[s3], *self.chip(0), ra2.at[s3, 0], ra2.at[s3, 1])
                 for d in PEERS:
-                    self.sub(d)[...] = fb[s3, :, self.relc(d)].astype(BF16)
+                    total(self.sub(d), fb.at[s3, :, self.relc(d)])
                 self.give(0, (1, -1))
             elif st == 4:
-                v = fb[s3, :, self.relc(0)]
-                for j in range(3):
-                    v = v + rb[s3, j].astype(F32)
-                self.sub(0)[...] = v.astype(BF16)
+                total(self.sub(0), fb.at[s3, :, self.relc(0)], rb.at[s3, 0], rb.at[s3, 1], rb.at[s3, 2])
                 self.give(1, PEERS)
             elif st == 5:
                 even = self.sub(0)[...].astype(F32) + rc[s6, 1].astype(F32)
@@ -244,7 +249,7 @@
             pl.semaphore_signal(free.at[2, 0, c.s6], inc=1, device_id={"dp": partner},
                                 device_id_type=pl.DeviceIdType.MESH)
             w.wait_recv()
-            c.block(2)[...] = c.chip(2).astype(BF16)
+            total(c.block(2), *c.chip(2))
             c.send(1)
 
         slot(t, t6, 1)

time: 152 us -> 150 us (0.987)
  Pallas kernels: 145 us -> 143 us
    pallas_call x1, Pallas kernels: 145 us -> 143 us  [local(): pl.pallas_call(kernel, out_shape=pltpu.VMEM((N, D, F), BF16), in_specs=[p...]
where the time goes in v3:
time: 150 us
  Pallas kernels  143 us (95%)
  local copies, waits for them, and re-layouts  6.68 us (4%)
    pallas_call x1, Pallas kernels, local(): pl.pallas_call(kernel, out_shape=pltpu.VMEM((N, D, F), BF16), in_specs=[p...  143 us
    unnamed x1, local copies, waits for them, and re-layouts  6.68 us

profile of v3, /device:TPU:1, one launch (start us, length us, event | category | flops | bytes accessed | tf_op | source)
XLA Modules:
  0.0 149.9 jit_solution(9140342630940456555)
XLA Ops:
  0.0 143.2 %wgrad_sum.1 = bf16[2,1280,3584]{2,1,0:T(8,128)(2,1)S(1)} custom-call(bf16[1,2,4096,1280]{3,2,1,0:T(8,128)(2,1)} %a_ref.1, bf16[1,2,4096,3584]{3,2,1,0:T(8,128)(2,1)} %g_ref.1), custom_call_target="tpu_custom_call" | custom-call | tf_op jit(solution)/shard_map/wgrad_sum/pallas_call | solution.py:271
  143.2 6.7 %copy.4 = bf16[2,1280,3584]{2,1,0:T(8,128)(2,1)} copy(bf16[2,1280,3584]{2,1,0:T(8,128)(2,1)S(1)} %wgrad_sum.1) | data formatting | bytes 36700160
